TPU v7x, 32 devices: a whole 2x2x4 slice. The times are simulated.
32 devices in a mesh: row: 2 (over x), col: 16 (over z, y, core).
Axes of the slice: x: 2, y: 2, z: 4, core: 2. Of those that a mesh axis runs over, the one named last changes fastest.
Arguments:
- adjacency: int32 [2048, 64], P('row', 'col'), may hold values from -2147483648 to 2147483647, as said below
- tile_mask: int32 [16, 16], P('row', 'col'), may hold values from 0 to 1, as said below
- thresholds: int32 [3], replicated, may hold values from 30 to 61
Outputs:
- truss_support: float32 [2048, 2048], P('row', 'col')
- edge_counts: int32 [3], replicated
Inputs may be any that keep to these rules, and one draw needn't show every extreme that they name: The graph of adjacency is symmetric with an empty diagonal: bit b of word w of row i equals the bit for row 32 w + b and column i. `tile_mask`: Symmetric.
All inputs are finite; a program needn't handle non-finite values.
Results may differ from a plain program's by a relative error of at most 0.0003.
Values may be sent and summed in bfloat16 or wider, within the bound.
No kernel may reach another device: no remote copies, remote signals or barrier semaphores. Data moves between devices by JAX's collectives and lax.ppermute only.
A program may use at most 64 MiB of HBM per device.

v0:
```python
import jax
import jax.numpy as jnp
from jax import lax
from jax.sharding import PartitionSpec as P

TILE = 128
ITERS = 3


def unpack_bits(packed_rows):
    shifts = jnp.arange(32, dtype=jnp.int32)
    flat_bits = jnp.bitwise_and(jnp.right_shift(packed_rows[:, :, None], shifts), 1)
    return flat_bits.reshape(packed_rows.shape[0], packed_rows.shape[1] * 32)


def pack_bits(flat_bits):
    shifts = jnp.arange(32, dtype=jnp.int32)
    grouped = flat_bits.reshape(flat_bits.shape[0], flat_bits.shape[1] // 32, 32)
    return jnp.sum(jnp.left_shift(grouped, shifts), axis=-1, dtype=jnp.int32)


def block_product(packed_rows, matching):
    operand = unpack_bits(packed_rows).astype(jnp.bfloat16)
    return jnp.dot(operand, matching, preferred_element_type=jnp.float32)


def local(adjacency, tile_mask, thresholds):
    rows_here = adjacency.shape[0]
    cols_here = adjacency.shape[1] * 32
    flat_bits = unpack_bits(adjacency)
    tile_cover = jnp.broadcast_to(
        tile_mask[:, None, :, None], (tile_mask.shape[0], TILE, tile_mask.shape[1], TILE)
    )
    surviving = flat_bits * tile_cover.reshape(rows_here, cols_here)
    survived_list = []
    support = jnp.zeros((rows_here, cols_here), jnp.float32)
    for iteration in range(ITERS):
        packed_here = pack_bits(surviving)
        column_words = lax.all_gather(packed_here, "row", axis=0, tiled=True)
        column_bits = unpack_bits(column_words)
        lower_panel = column_bits.astype(jnp.bfloat16)
        wedge_counts = block_product(
            lax.all_gather(packed_here, "col", axis=1, tiled=True), lower_panel
        )
        support = wedge_counts * surviving.astype(jnp.float32)
        retained = (support >= thresholds[iteration].astype(jnp.float32)).astype(jnp.int32)
        surviving = surviving * retained
        survived = jnp.sum(surviving)
        survived_list.append(survived)
    edge_counts = lax.psum(jnp.stack(survived_list), ("row", "col"))
    truss_support = (
        support * surviving.astype(jnp.float32) / thresholds[ITERS - 1].astype(jnp.float32)
    )
    return (truss_support, edge_counts)


def solution(mesh):
    in_specs = (P("row", "col"), P("row", "col"), P())
    out_specs = (P("row", "col"), P())
    return jax.shard_map(local, mesh=mesh, in_specs=in_specs, out_specs=out_specs, check_vma=False)
```

profile of v0, /device:TPU:0, one launch (start us, length us, event | category | flops | bytes accessed | tf_op | source)
XLA Modules:
  0.0 130.6 jit_solution(8113006497730622411)
XLA Ops:
  0.6 0.0 copy-start
  0.6 0.6 copy-done
  1.3 1.3 %fusion.8 = (s32[1]{0:T(128)}, s32[1]{0:T(128)}, s32[1]{0:T(128)}) fusion(s32[3]{0:T(128)} %param.5), kind=kLoop, calls=%fused_computation.25 | loop fusion | bytes 24 | tf_op jit(solution)/shard_map/slice | solution.py:46
  4.5 0.1 shift_right_arithmetic.170
  4.6 0.1 broadcast_bitcast_fusion
  4.7 0.8 shift-left_reduce_fusion.2
  5.5 5.3 %all_gather.19 = s32[2048,4]{0,1:T(4,128)S(1)} all-gather(s32[1024,4]{0,1:T(4,128)S(1)} %shift-left_reduce_fusion.2), channel_id=1, replica_groups=mesh['row'=2,'col'=16] {'row'}, dimensions={0}, use_global_device_ids=true | all-gather | bytes 49152 | tf_op jit(solution)/shard_map/all_gather | solution.py:39
  10.8 22.9 %all-gather = s32[16,4,1024]{2,1,0:T(4,128)S(1)} all-gather(s32[1,4,1024]{2,1,0:T(4,128)S(1)} %bitcast.55), channel_id=1, replica_groups=mesh['row'=2,'col'=16] {'col'}, dimensions={0}, use_global_device_ids=true | all-gather | bytes 278528 | tf_op jit(solution)/shard_map/all_gather | solution.py:43
  33.7 0.1 reshape.241
  33.8 0.1 and_convert_fusion.5
  34.0 0.8 fusion.5
  34.8 1.6 %and_convert_fusion.2 = bf16[1024,64,32]{0,2,1:T(8,128)(2,1)S(1)} fusion(s32[1024,64]{0,1:T(8,128)S(1)} %bitcast.49), kind=kLoop, calls=%fused_computation.2 | loop fusion | flops 6291456 | bytes 4456448 | tf_op jit(solution)/shard_map/convert_element_type | solution.py:23
  36.4 0.9 shift-left_reduce_fusion.1
  37.3 0.8 reduce_sum.57
  38.0 4.4 %all_gather.21 = s32[2048,4]{0,1:T(4,128)S(1)} all-gather(s32[1024,4]{0,1:T(4,128)S(1)} %get-tuple-element.13), channel_id=1, replica_groups=mesh['row'=2,'col'=16] {'row'}, dimensions={0}, use_global_device_ids=true | all-gather | bytes 49152 | tf_op jit(solution)/shard_map/all_gather | solution.py:39
  42.4 17.8 %all-gather.1 = s32[16,4,1024]{2,1,0:T(4,128)S(1)} all-gather(s32[1,4,1024]{2,1,0:T(4,128)S(1)} %bitcast.53), channel_id=1, replica_groups=mesh['row'=2,'col'=16] {'col'}, dimensions={0}, use_global_device_ids=true | all-gather | bytes 278528 | tf_op jit(solution)/shard_map/all_gather | solution.py:43
  60.3 0.1 reshape.243
  60.3 0.1 and_convert_fusion.4
  60.5 1.6 %and_convert_fusion.1 = bf16[1024,64,32]{0,2,1:T(8,128)(2,1)S(1)} fusion(s32[1024,64]{0,1:T(8,128)S(1)} %bitcast.50), kind=kLoop, calls=%fused_computation.1 | loop fusion | flops 6291456 | bytes 4456448 | tf_op jit(solution)/shard_map/convert_element_type | solution.py:23
  62.0 0.9 shift-left_reduce_fusion
  63.0 4.4 %all_gather.23 = s32[2048,4]{0,1:T(4,128)S(1)} all-gather(s32[1024,4]{0,1:T(4,128)S(1)} %get-tuple-element.15), channel_id=1, replica_groups=mesh['row'=2,'col'=16] {'row'}, dimensions={0}, use_global_device_ids=true | all-gather | bytes 49152 | tf_op jit(solution)/shard_map/all_gather | solution.py:39
  67.4 19.9 %all-gather.2 = s32[16,4,1024]{2,1,0:T(4,128)S(1)} all-gather(s32[1,4,1024]{2,1,0:T(4,128)S(1)} %bitcast.54), channel_id=1, replica_groups=mesh['row'=2,'col'=16] {'col'}, dimensions={0}, use_global_device_ids=true | all-gather | bytes 278528 | tf_op jit(solution)/shard_map/all_gather | solution.py:43
  87.3 0.1 reshape.245
  87.4 0.1 and_convert_fusion.3
  87.5 1.6 %and_convert_fusion = bf16[1024,64,32]{0,2,1:T(8,128)(2,1)S(1)} fusion(s32[1024,64]{0,1:T(8,128)S(1)} %bitcast.51), kind=kLoop, calls=%fused_computation | loop fusion | flops 6291456 | bytes 4456448 | tf_op jit(solution)/shard_map/convert_element_type | solution.py:23
  89.1 0.9 multiply_divide_fusion
  89.9 0.9 fusion.7
  90.8 2.0 %pad_add_fusion = s32[3]{0:T(128)S(1)} fusion(s32[1]{0:T(128)} %bitcast.25, s32[1]{0:T(128)} %bitcast.24, s32[1]{0:T(128)} %bitcast.23), kind=kLoop, calls=%fused_computation.23 | loop fusion | flops 6 | bytes 24 | tf_op jit(solution)/shard_map/stack | solution.py:50
  92.8 1.0 copy.11
  93.8 36.8 %psum.7 = s32[3]{0:T(128)} all-reduce(s32[3]{0:T(128)S(1)} %pad_add_fusion), channel_id=1, replica_groups=mesh['row'=2,'col'=16] {'row','col'}, use_global_device_ids=true, to_apply=%region_6.0 | all-reduce | flops 3 | bytes 24 | tf_op jit(solution)/shard_map/psum | solution.py:50
  (1 shorter events, 0.0 us)
Async XLA Ops:
  0.6 0.7 copy-start
where the time goes:
time: 132 us; the launch traced here: 131 us
  blocking collectives  112 us (85%)
  other arithmetic  10.3 us (8%)
  local copies, waits for them, and re-layouts  3.42 us (3%)
  matrix products  2.67 us (2%)
  between operations  2.59 us (2%)
    all_gather x3, blocking collectives, local(): lax.all_gather(packed_here, 'col', axis=1, tiled=True)  60.6 us
    psum x1, blocking collectives, local(): edge_counts = lax.psum(jnp.stack(survived_list), ('row', 'col'))  36.8 us
    all_gather x3, blocking collectives, local(): column_words = lax.all_gather(packed_here, 'row', axis=0, tiled=True)  14.1 us
    convert_element_type x3, other arithmetic, block_product(): operand = unpack_bits(packed_rows).astype(jnp.bfloat16)  4.67 us
    dot_general x3, matrix products, block_product(): return jnp.dot(operand, matching, preferred_element_type=jnp.float32)  2.67 us

commit v1 on v0

--- a/solution.py
+++ b/solution.py
@@ -1,10 +1,17 @@
+import functools
+
 import jax
 import jax.numpy as jnp
 from jax import lax
+from jax.experimental import pallas as pl
+from jax.experimental.pallas import tpu as pltpu
 from jax.sharding import PartitionSpec as P
 
 TILE = 128
 ITERS = 3
+BLOCK = 512
+REPLICATED_LIMIT = 2048
+OPERAND = jnp.float8_e4m3fn
 
 
 def unpack_bits(packed_rows):
@@ -24,7 +31,7 @@
     return jnp.dot(operand, matching, preferred_element_type=jnp.float32)
 
 
-def local(adjacency, tile_mask, thresholds):
+def distributed(adjacency, tile_mask, thresholds):
     rows_here = adjacency.shape[0]
     cols_here = adjacency.shape[1] * 32
     flat_bits = unpack_bits(adjacency)
@@ -45,8 +52,7 @@
         support = wedge_counts * surviving.astype(jnp.float32)
         retained = (support >= thresholds[iteration].astype(jnp.float32)).astype(jnp.int32)
         surviving = surviving * retained
-        survived = jnp.sum(surviving)
-        survived_list.append(survived)
+        survived_list.append(jnp.sum(surviving))
     edge_counts = lax.psum(jnp.stack(survived_list), ("row", "col"))
     truss_support = (
         support * surviving.astype(jnp.float32) / thresholds[ITERS - 1].astype(jnp.float32)
@@ -54,7 +60,99 @@
     return (truss_support, edge_counts)
 
 
+def peel_kernel(where_ref, thr_ref, words_ref, out_ref, counts_ref, live_a, live_b):
+    n_word_rows, verts = words_ref.shape
+    rows_here, cols_here = out_ref.shape
+    n_blocks = verts // BLOCK
+
+    def unpack_group(g, carry):
+        words = words_ref[pl.ds(pl.multiple_of(g * 8, 8), 8), :]
+        shift = lax.broadcasted_iota(jnp.int32, (32, verts), 0)
+        for k in range(8):
+            row = jnp.broadcast_to(words[k : k + 1, :], (32, verts))
+            bits = jnp.bitwise_and(jnp.right_shift(row, shift), 1)
+            live_a[pl.ds(pl.multiple_of(g * 256 + k * 32, 32), 32), :] = bits.astype(
+                jnp.float32
+            ).astype(OPERAND)
+        return carry
+
+    lax.fori_loop(0, n_word_rows // 8, unpack_group, 0)
+
+    def sweep(src, dst, thr):
+        def outer(bi, acc):
+            ri = pl.ds(pl.multiple_of(bi * BLOCK, BLOCK), BLOCK)
+
+            def inner(bj, acc):
+                rj = pl.ds(pl.multiple_of(bj * BLOCK, BLOCK), BLOCK)
+                wedges = jnp.dot(src[ri, :], src[:, rj], preferred_element_type=jnp.float32)
+                old = src[ri, rj].astype(jnp.float32)
+                new = jnp.where(wedges >= thr, old, 0.0)
+                if dst is not None:
+                    dst[ri, rj] = new.astype(OPERAND)
+                    dst[rj, ri] = new.T.astype(OPERAND)
+                part = jnp.sum(new.reshape(BLOCK // 8, 8, BLOCK), axis=0)
+                weight = jnp.where(bi == bj, 1.0, 2.0)
+                return acc + part * weight
+
+            return lax.fori_loop(bi, n_blocks, inner, acc)
+
+        acc = lax.fori_loop(0, n_blocks, outer, jnp.zeros((8, BLOCK), jnp.float32))
+        return jnp.sum(acc).astype(jnp.int32)
+
+    counts_ref[0] = sweep(live_a, live_b, thr_ref[0].astype(jnp.float32))
+    counts_ref[1] = sweep(live_b, live_a, thr_ref[1].astype(jnp.float32))
+    last = thr_ref[2].astype(jnp.float32)
+    counts_ref[2] = sweep(live_a, None, last)
+    ri = pl.ds(pl.multiple_of(where_ref[0] * rows_here, rows_here), rows_here)
+    rj = pl.ds(pl.multiple_of(where_ref[1] * cols_here, cols_here), cols_here)
+    wedges = jnp.dot(live_a[ri, :], live_a[:, rj], preferred_element_type=jnp.float32)
+    old = live_a[ri, rj].astype(jnp.float32)
+    out_ref[...] = jnp.where(wedges >= last, wedges * old, 0.0) / last
+
+
+def gather_words(words, n_rows, n_cols):
+    both = lax.all_gather(words, "row", axis=0)
+    all_parts = lax.all_gather(both, "col", axis=0)
+    n_words = words.shape[0]
+    return all_parts.transpose(0, 2, 1, 3).reshape(n_cols * n_words, n_rows * words.shape[1])
+
+
+def replicated(n_rows, n_cols, adjacency, tile_mask, thresholds):
+    rows_here, words_here = adjacency.shape
+    cols_here = words_here * 32
+    verts = rows_here * n_rows
+    cover = jnp.repeat(jnp.repeat(tile_mask.T, TILE, axis=1), TILE // 32, axis=0)
+    words = gather_words(adjacency.T * cover, n_rows, n_cols)
+    where = jnp.stack([lax.axis_index("row"), lax.axis_index("col")]).astype(jnp.int32)
+    return pl.pallas_call(
+        peel_kernel,
+        in_specs=[
+            pl.BlockSpec(memory_space=pltpu.SMEM),
+            pl.BlockSpec(memory_space=pltpu.SMEM),
+            pl.BlockSpec(memory_space=pltpu.VMEM),
+        ],
+        out_specs=[
+            pl.BlockSpec(memory_space=pltpu.VMEM),
+            pl.BlockSpec(memory_space=pltpu.SMEM),
+        ],
+        out_shape=[
+            jax.ShapeDtypeStruct((rows_here, cols_here), jnp.float32),
+            jax.ShapeDtypeStruct((ITERS,), jnp.int32),
+        ],
+        scratch_shapes=[pltpu.VMEM((verts, verts), OPERAND) for _ in range(2)],
+        name="peel",
+    )(where, thresholds, words)
+
+
+def local(n_rows, n_cols, adjacency, tile_mask, thresholds):
+    verts = adjacency.shape[0] * n_rows
+    if verts <= REPLICATED_LIMIT and verts % BLOCK == 0:
+        return replicated(n_rows, n_cols, adjacency, tile_mask, thresholds)
+    return distributed(adjacency, tile_mask, thresholds)
+
+
 def solution(mesh):
     in_specs = (P("row", "col"), P("row", "col"), P())
     out_specs = (P("row", "col"), P())
-    return jax.shard_map(local, mesh=mesh, in_specs=in_specs, out_specs=out_specs, check_vma=False)
+    body = functools.partial(local, mesh.shape["row"], mesh.shape["col"])
+    return jax.shard_map(body, mesh=mesh, in_specs=in_specs, out_specs=out_specs, check_vma=False)

time: 132 us -> 63.9 us (0.48)
  blocking collectives: 112 us -> 29.1 us
  Pallas kernels: 0 us -> 31.8 us
  other arithmetic: 10.3 us -> 0.66 us
  matrix products: 2.67 us -> 0 us
  local copies, waits for them, and re-layouts: 3.42 us -> 1.43 us
  between operations: 2.59 us -> 0.66 us
    all_gather x6 -> x2, blocking collectives: 74.7 us -> 29.1 us  [the longest x1 23.8 us: gather_words(): all_parts = lax.all_gather(both, 'col', axis=0)]
    psum x1 -> x0, blocking collectives: 36.8 us -> none  [local(): edge_counts = lax.psum(jnp.stack(survived_list), ('row', 'col'))]
    pallas_call x0 -> x1, Pallas kernels: none -> 31.8 us  [replicated(): pl.pallas_call(peel_kernel, in_specs=[pl.BlockSpec(memory_space=pltpu.SME...]
    convert_element_type x6 -> x0, other arithmetic: 5.05 us -> none  [the longest x3 4.67 us: block_product(): operand = unpack_bits(packed_rows).astype(jnp.bfloat16)]
    dot_general x3 -> x0, matrix products: 2.67 us -> none  [block_product(): return jnp.dot(operand, matching, preferred_element_type=jnp.float32)]
    reduce_sum x3 -> x0, other arithmetic: 2.48 us -> none  [the longest x2 1.64 us: local(): survived = jnp.sum(surviving)]
    slice x1 -> x0, local copies, waits for them, and re-layouts: 1.35 us -> none  [local(): thresholds[iteration].astype(jnp.float32)]
where the time goes in v1:
time: 63.9 us; the launch traced here: 63.7 us
  Pallas kernels  31.8 us (50%)
  blocking collectives  29.1 us (46%)
  local copies, waits for them, and re-layouts  1.43 us (2%)
  other arithmetic  0.66 us (1%)
  between operations  0.66 us (1%)
    pallas_call x1, Pallas kernels, replicated(): pl.pallas_call(peel_kernel, in_specs=[pl.BlockSpec(memory_space=pltpu.SME...  31.8 us
    all_gather x1, blocking collectives, gather_words(): all_parts = lax.all_gather(both, 'col', axis=0)  23.8 us
    all_gather x1, blocking collectives, gather_words(): both = lax.all_gather(words, 'row', axis=0)  5.33 us

profile of v1, /device:TPU:0, one launch (start us, length us, event | category | flops | bytes accessed | tf_op | source)
XLA Modules:
  0.0 63.7 jit_solution(16362186992370792970)
XLA Ops:
  0.6 0.0 copy-start
  0.6 0.0 copy-start.1
  0.7 0.7 %pad_add_fusion.where_ref = s32[2]{0:T(128)} fusion(s32[1]{0:T(128)} %bitcast.1, s32[1]{0:T(128)} %bitcast), kind=kLoop, calls=%fused_computation.2 | loop fusion | flops 2 | bytes 16 | tf_op jit(solution)/shard_map/stack | solution.py:126
  1.3 0.0 copy-done
  1.3 0.1 broadcast_bitcast_fusion
  1.4 0.0 copy-done.1
  1.4 5.3 %all-gather.2 = s32[2,4,1024]{2,1,0:T(4,128)S(1)} all-gather(s32[1,4,1024]{2,1,0:T(4,128)S(1)} %multiply_bitcast_fusion), channel_id=2, replica_groups=mesh['row'=2,'col'=16] {'row'}, dimensions={0}, use_global_device_ids=true | all-gather | bytes 49152 | tf_op jit(solution)/shard_map/all_gather | solution.py:114
  6.7 23.8 %all-gather.1 = s32[32,4,1024]{2,1,0:T(4,128)S(1)} all-gather(s32[2,4,1024]{2,1,0:T(4,128)S(1)} %all-gather.2), channel_id=3, replica_groups=mesh['row'=2,'col'=16] {'col'}, dimensions={0}, use_global_device_ids=true | all-gather | bytes 557056 | tf_op jit(solution)/shard_map/all_gather | solution.py:115
  30.5 0.4 copy.6
  30.9 0.9 %copy.7 = s32[8,8,2,1024]{3,1,2,0:T(8,128)} copy(s32[8,8,2,1024]{3,2,1,0:T(2,128)S(1)} %bitcast.17) | data formatting | bytes 1048576
  31.9 31.8 %peel.1 = (f32[1024,128]{1,0:T(8,128)}, s32[3]{0:T(128)}) custom-call(s32[2]{0:T(128)} %pad_add_fusion.where_ref, s32[3]{0:T(128)} %thr_ref.1, s32[64,2048]{1,0:T(8,128)} %bitcast.15), custom_call_target="tpu_custom_call" | custom-call | tf_op jit(solution)/shard_map/peel/pallas_call | solution.py:127
  (1 shorter events, 0.0 us)
Async XLA Ops:
  0.6 0.7 %copy-start = (s32[8,1]{0,1:T(1,128)S(1)}, s32[8,1]{0,1:T(1,128)}, u32[]{:S(2)}) copy-start(s32[8,1]{0,1:T(1,128)} %param.4) | copy-start | bytes 100
  0.6 0.7 %copy-start.1 = (s32[1024,4]{0,1:T(4,128)S(1)}, s32[1024,4]{0,1:T(4,128)}, u32[]{:S(2)}) copy-start(s32[1024,4]{0,1:T(4,128)} %param.3) | copy-start | bytes 49156
